TPU v7x, 32 devices: a whole 2x2x4 slice. The times are simulated.
32 devices in a mesh: path: 16 (over z, x, core), shard: 2 (over y).
Axes of the slice: x: 2, y: 2, z: 4, core: 2. Of those that a mesh axis runs over, the one named last changes fastest.
Arguments:
- deltas: bfloat16 [16, 32, 4096], P('path', 'shard'), may hold values from -96 to 96
- momentum: float32 [16, 32, 4096], P(None, 'shard', 'path'), may hold values from -4 to 4
- path_module: int32 [16], replicated, may hold values from 0 to 15, as said below
Outputs:
- path_update: bfloat16 [16, 32, 4096], P('path', 'shard')
- new_momentum: float32 [16, 32, 4096], P(None, 'shard', 'path')
Inputs may be any that keep to these rules, and one draw needn't show every extreme that they name: `path_module`: every module is used by at least one and at most seven paths.
All inputs are finite; a program needn't handle non-finite values.
Results may differ from a plain program's by a relative error of at most 0.0004.
Values may be sent and summed in bfloat16 or wider, within the bound.
A program may use at most 64 MiB of HBM per device.

v0:
```python
import jax
import jax.numpy as jnp
from jax import lax
from jax.sharding import PartitionSpec as P

D = 4096
outer_rate = 0.7
momentum_rate = 0.9
clip_ratio = 2.0


def local(deltas, momentum, path_module):
    own_index = lax.axis_index("path")
    modules = momentum.shape[0]
    row_count = deltas.shape[1]
    onehot = (path_module[:, None] == jnp.arange(modules, dtype=jnp.int32)[None, :]).astype(
        jnp.float32
    )
    counts = jnp.sum(onehot, axis=0)
    own_module = lax.dynamic_index_in_dim(path_module, own_index, 0, keepdims=False)
    column_pieces = lax.all_to_all(deltas, "path", split_axis=2, concat_axis=0, tiled=True)
    totals = jnp.einsum(
        "pm,prc->mrc",
        onehot.astype(jnp.bfloat16),
        column_pieces,
        preferred_element_type=jnp.float32,
    )
    outer_grad = totals / counts[:, None, None]
    local_squares = jnp.sum(outer_grad * outer_grad, axis=(1, 2))
    norm_squares = lax.psum(local_squares, ("path", "shard"))
    limit = clip_ratio * jnp.sqrt(jnp.float32(row_count * lax.axis_size("shard") * D))
    shrink = jnp.minimum(1.0, limit / jnp.sqrt(norm_squares + 1e-06))
    clipped = outer_grad * shrink[:, None, None]
    new_momentum = momentum_rate * momentum + clipped
    outer_step = (outer_rate * (clipped + momentum_rate * new_momentum)).astype(jnp.bfloat16)
    gathered = lax.all_gather(outer_step, "path", axis=2, tiled=True)
    path_update = lax.dynamic_index_in_dim(gathered, own_module, 0, keepdims=True)
    return (path_update, new_momentum)


def solution(mesh):
    return jax.shard_map(
        local,
        mesh=mesh,
        in_specs=(P("path", "shard", None), P(None, "shard", "path"), P()),
        out_specs=(P("path", "shard", None), P(None, "shard", "path")),
        check_vma=False,
    )
```

profile of v0, /device:TPU:0, one launch (start us, length us, event | category | flops | bytes accessed | tf_op | source)
XLA Modules:
  0.0 145.2 jit_solution(7055501070345371449)
XLA Ops:
  7.2 4.3 %copy.8 = bf16[1,16,4096]{1,0,2:T(2,128)(2,1)S(1)} copy(bf16[1,16,4096]{2,1,0:T(8,128)(2,1)} %param.3) | data formatting | bytes 262144 | tf_op args[0]
  11.5 0.5 broadcast.26
  12.0 0.0 copy-start.1
  12.0 22.4 %reduce = bf16[4096,16]{1,0:T(8,128)(2,1)S(1)} reduce(bf16[4096,1,16]{2,1,0:T(2,128)(2,1)S(1)} %bitcast.25, bf16[]{:T(256)} %broadcast.26), dimensions={1}, to_apply=%bitcast.15.reduce_sub_computation | reduce | bytes 262146
  34.4 1.8 %reshape.8 = bf16[16,2,2048]{2,1,0:T(2,128)(2,1)} reshape(bf16[4096,16]{1,0:T(8,128)(2,1)S(1)} %reduce) | data formatting | bytes 262144
  36.2 7.4 %all-to-all-start = ((bf16[16,2,2048]{2,1,0:T(2,128)(2,1)}), bf16[16,2,2048]{2,1,0:T(2,128)(2,1)S(1)}, u32[]{:S(2)}, u32[]{:S(2)}) async-start(bf16[16,2,2048]{2,1,0:T(2,128)(2,1)} %reshape.8), calls=%async_computation | async-start | bytes 262144 | tf_op jit(solution)/shard_map/all_to_all | solution.py:21
  43.6 0.0 all-gather.2.cloned.1.call-start
  43.6 0.0 copy-done.1
  43.6 0.1 convert_reduce_fusion
  43.8 7.7 %all-to-all-done = bf16[16,2,2048]{2,1,0:T(2,128)(2,1)S(1)} async-done(((bf16[16,2,2048]{2,1,0:T(2,128)(2,1)}), bf16[16,2,2048]{2,1,0:T(2,128)(2,1)S(1)}, u32[]{:S(2)}, u32[]{:S(2)}) %all-to-all-start) | async-done | bytes 131104 | tf_op jit(solution)/shard_map/all_to_all | solution.py:21
  51.5 1.8 %reshape.9 = bf16[4096,1,16]{2,1,0:T(2,128)(2,1)S(1)} reshape(bf16[16,2,2048]{2,1,0:T(2,128)(2,1)S(1)} %all-to-all-done) | data formatting | bytes 262144
  53.3 0.0 copy-start
  53.3 2.0 %copy.9 = bf16[1,16,4096]{2,1,0:T(8,128)(2,1)S(1)} copy(bf16[1,16,4096]{1,0,2:T(2,128)(2,1)S(1)} %bitcast.26) | data formatting | bytes 262144 | tf_op jit(solution)/shard_map/all_to_all | solution.py:21
  55.3 0.3 multiply_reduce_fusion
  55.6 37.5 %psum.7 = f32[16]{0:T(128)S(1)} all-reduce(f32[16]{0:T(128)S(1)} %get-tuple-element.8), channel_id=1, replica_groups=mesh['path'=16,'shard'=2] {'path','shard'}, use_global_device_ids=true, to_apply=%region_2.3 | all-reduce | flops 16 | bytes 128 | tf_op jit(solution)/shard_map/psum | solution.py:30
  93.1 0.0 copy-done
  93.1 0.9 fusion
  94.0 0.0 all-gather.2.cloned.1.call-update
  94.0 0.6 dynamic_slice.8
  96.5 0.9 copy.12
  97.4 38.6 %all-gather.2.cloned.1.call-done = bf16[16,16,4096]{2,0,1:T(8,128)(2,1)} async-done(((bf16[16,16,256]{2,0,1:T(8,128)(2,1)}), bf16[16,16,4096]{2,0,1:T(8,128)(2,1)}) %all-gather.2.cloned.1.call-update) | async-done | bytes 2097168 | tf_op jit(solution)/shard_map/all_gather | solution.py:36
  136.0 1.5 %constant_dynamic-slice_fusion = bf16[1,16,4096]{2,0,1:T(2,128)(2,1)S(1)} fusion(bf16[16,16,4096]{2,0,1:T(8,128)(2,1)} %all-gather.2.cloned.1.call-done, s32[]{:T(128)S(6)} %select_n.9), kind=kLoop, calls=%fused_computation.12 | loop fusion | bytes 262148 | tf_op jit(solution)/shard_map/jit(dynamic_index_in_dim)/dynamic_slice | solution.py:37
  137.5 0.8 copy.11
  (2 shorter events, 0.0 us)
Async XLA Ops:
  12.0 31.6 %copy-start.1 = (s32[16]{0:T(128)S(1)}, s32[16]{0:T(128)}, u32[]{:S(2)}) copy-start(s32[16]{0:T(128)} %param.5) | copy-start | bytes 196
  36.2 15.3 %all-to-all-start = ((bf16[16,2,2048]{2,1,0:T(2,128)(2,1)}), bf16[16,2,2048]{2,1,0:T(2,128)(2,1)S(1)}, u32[]{:S(2)}, u32[]{:S(2)}) async-start(bf16[16,2,2048]{2,1,0:T(2,128)(2,1)} %reshape.8), calls=%async_computation | async-start | bytes 262144 | tf_op jit(solution)/shard_map/all_to_all | solution.py:21
  43.6 92.4 %all-gather.2.cloned.1.call-start = ((), (), s32[]{:S(2)}) async-start(), calls=%async_computation.1 | async-start | bytes 2228224 | tf_op jit(solution)/shard_map/all_gather | solution.py:36
  53.3 39.8 %copy-start = (f32[16,16,256]{2,1,0:T(8,128)S(1)}, f32[16,16,256]{2,1,0:T(8,128)}, u32[]{:S(2)}) copy-start(f32[16,16,256]{2,1,0:T(8,128)} %param.4) | copy-start | bytes 786436
Sparse Core Ops, SparseCore 0:
  94.1 41.7 all-gather.1
where the time goes:
time: 146 us; the launch traced here: 145 us
  waiting for transfers between devices  46.3 us (32%)
  blocking collectives  37.5 us (26%)
  other arithmetic  23.4 us (16%)
  between operations  16 us (11%)
  local copies, waits for them, and re-layouts  14.2 us (10%)
  starting transfers between devices  7.43 us (5%)
    all_gather x1, waiting for transfers between devices, local(): gathered = lax.all_gather(outer_step, 'path', axis=2, tiled=True)  38.6 us
    psum x1, blocking collectives, local(): norm_squares = lax.psum(local_squares, ('path', 'shard'))  37.5 us
    unnamed x1, other arithmetic  22.4 us
    unnamed x11, local copies, waits for them, and re-layouts  10.1 us
    all_to_all x1, waiting for transfers between devices, local(): lax.all_to_all(deltas, 'path', split_axis=2, concat_axis=0, tiled=True)  7.73 us
    all_to_all x1, starting transfers between devices, local(): lax.all_to_all(deltas, 'path', split_axis=2, concat_axis=0, tiled=True)  7.39 us
  transfers between devices with their start and end apart: 2, of which 2 were waited for; matrix products, arithmetic and copies ran while one was open for 1% of the time, Pallas kernels for 0%

commit v1 on v0

--- a/solution.py
+++ b/solution.py
@@ -27,7 +27,7 @@
     )
     outer_grad = totals / counts[:, None, None]
     local_squares = jnp.sum(outer_grad * outer_grad, axis=(1, 2))
-    norm_squares = lax.psum(local_squares, ("path", "shard"))
+    norm_squares = lax.psum(lax.psum(local_squares, axis_name="shard"), "path")
     limit = clip_ratio * jnp.sqrt(jnp.float32(row_count * lax.axis_size("shard") * D))
     shrink = jnp.minimum(1.0, limit / jnp.sqrt(norm_squares + 1e-06))
     clipped = outer_grad * shrink[:, None, None]

time: 146 us -> 139 us (0.952)
  waiting for transfers between devices: 46.3 us -> 42.8 us
  blocking collectives: 37.5 us -> 34.4 us
    all_gather x1, waiting for transfers between devices: 38.6 us -> 35.1 us  [local(): gathered = lax.all_gather(outer_step, 'path', axis=2, tiled=True)]
    psum x1 -> x2, blocking collectives: 37.5 us -> 34.4 us  [local(): norm_squares = lax.psum(lax.psum(local_squares, axis_name='shard'), 'path')]
where the time goes in v1:
time: 139 us
  waiting for transfers between devices  42.8 us (31%)
  blocking collectives  34.4 us (25%)
  other arithmetic  23.4 us (17%)
  between operations  16 us (12%)
  local copies, waits for them, and re-layouts  14.2 us (10%)
  starting transfers between devices  7.43 us (5%)
    all_gather x1, waiting for transfers between devices, local(): gathered = lax.all_gather(outer_step, 'path', axis=2, tiled=True)  35.1 us
    psum x2, blocking collectives, local(): norm_squares = lax.psum(lax.psum(local_squares, axis_name='shard'), 'path')  34.4 us
    unnamed x1, other arithmetic  22.4 us
    unnamed x11, local copies, waits for them, and re-layouts  10.1 us
    all_to_all x1, waiting for transfers between devices, local(): lax.all_to_all(deltas, 'path', split_axis=2, concat_axis=0, tiled=True)  7.73 us
    all_to_all x1, starting transfers between devices, local(): lax.all_to_all(deltas, 'path', split_axis=2, concat_axis=0, tiled=True)  7.39 us
  transfers between devices with their start and end apart: 2, of which 2 were waited for; matrix products, arithmetic and copies ran while one was open for 1% of the time, Pallas kernels for 0%

profile of v1, /device:TPU:0, one launch (start us, length us, event | category | flops | bytes accessed | tf_op | source)
XLA Modules:
  0.0 138.6 jit_solution(5257436493762257069)
XLA Ops:
  7.2 4.3 %copy.8 = bf16[1,16,4096]{1,0,2:T(2,128)(2,1)S(1)} copy(bf16[1,16,4096]{2,1,0:T(8,128)(2,1)} %param.3) | data formatting | bytes 262144 | tf_op args[0]
  11.5 0.5 broadcast.26
  12.0 0.0 copy-start.1
  12.0 22.4 %reduce = bf16[4096,16]{1,0:T(8,128)(2,1)S(1)} reduce(bf16[4096,1,16]{2,1,0:T(2,128)(2,1)S(1)} %bitcast.25, bf16[]{:T(256)} %broadcast.26), dimensions={1}, to_apply=%bitcast.15.reduce_sub_computation | reduce | bytes 262146
  34.4 1.8 %reshape.8 = bf16[16,2,2048]{2,1,0:T(2,128)(2,1)} reshape(bf16[4096,16]{1,0:T(8,128)(2,1)S(1)} %reduce) | data formatting | bytes 262144
  36.2 7.4 %all-to-all-start = ((bf16[16,2,2048]{2,1,0:T(2,128)(2,1)}), bf16[16,2,2048]{2,1,0:T(2,128)(2,1)S(1)}, u32[]{:S(2)}, u32[]{:S(2)}) async-start(bf16[16,2,2048]{2,1,0:T(2,128)(2,1)} %reshape.8), calls=%async_computation | async-start | bytes 262144 | tf_op jit(solution)/shard_map/all_to_all | solution.py:21
  43.6 0.0 all-gather.2.cloned.1.call-start
  43.6 0.0 copy-done.1
  43.6 0.1 convert_reduce_fusion
  43.8 7.7 %all-to-all-done = bf16[16,2,2048]{2,1,0:T(2,128)(2,1)S(1)} async-done(((bf16[16,2,2048]{2,1,0:T(2,128)(2,1)}), bf16[16,2,2048]{2,1,0:T(2,128)(2,1)S(1)}, u32[]{:S(2)}, u32[]{:S(2)}) %all-to-all-start) | async-done | bytes 131104 | tf_op jit(solution)/shard_map/all_to_all | solution.py:21
  51.5 1.8 %reshape.9 = bf16[4096,1,16]{2,1,0:T(2,128)(2,1)S(1)} reshape(bf16[16,2,2048]{2,1,0:T(2,128)(2,1)S(1)} %all-to-all-done) | data formatting | bytes 262144
  53.3 0.0 copy-start
  53.3 2.0 %copy.9 = bf16[1,16,4096]{2,1,0:T(8,128)(2,1)S(1)} copy(bf16[1,16,4096]{1,0,2:T(2,128)(2,1)S(1)} %bitcast.26) | data formatting | bytes 262144 | tf_op jit(solution)/shard_map/all_to_all | solution.py:21
  55.3 0.3 multiply_reduce_fusion
  55.6 4.9 %psum.14 = f32[16]{0:T(128)S(1)} all-reduce(f32[16]{0:T(128)S(1)} %get-tuple-element.8), channel_id=1, replica_groups=mesh['path'=16,'shard'=2] {'shard'}, use_global_device_ids=true, to_apply=%region_2.3 | all-reduce | flops 16 | bytes 128 | tf_op jit(solution)/shard_map/psum | solution.py:30
  60.5 29.5 %psum.15 = f32[16]{0:T(128)S(1)} all-reduce(f32[16]{0:T(128)S(1)} %psum.14), channel_id=1, replica_groups=mesh['path'=16,'shard'=2] {'path'}, use_global_device_ids=true, to_apply=%region_3.4 | all-reduce | flops 16 | bytes 128 | tf_op jit(solution)/shard_map/psum | solution.py:30
  90.0 0.0 copy-done
  90.0 0.9 fusion
  90.9 0.0 all-gather.2.cloned.1.call-update
  90.9 0.6 dynamic_slice.8
  93.5 0.9 copy.12
  94.3 35.1 %all-gather.2.cloned.1.call-done = bf16[16,16,4096]{2,0,1:T(8,128)(2,1)} async-done(((bf16[16,16,256]{2,0,1:T(8,128)(2,1)}), bf16[16,16,4096]{2,0,1:T(8,128)(2,1)}) %all-gather.2.cloned.1.call-update) | async-done | bytes 2097168 | tf_op jit(solution)/shard_map/all_gather | solution.py:36
  129.4 1.5 %constant_dynamic-slice_fusion = bf16[1,16,4096]{2,0,1:T(2,128)(2,1)S(1)} fusion(bf16[16,16,4096]{2,0,1:T(8,128)(2,1)} %all-gather.2.cloned.1.call-done, s32[]{:T(128)S(6)} %select_n.9), kind=kLoop, calls=%fused_computation.12 | loop fusion | bytes 262148 | tf_op jit(solution)/shard_map/jit(dynamic_index_in_dim)/dynamic_slice | solution.py:37
  131.0 0.8 copy.11
  (2 shorter events, 0.0 us)
Async XLA Ops:
  12.0 31.6 %copy-start.1 = (s32[16]{0:T(128)S(1)}, s32[16]{0:T(128)}, u32[]{:S(2)}) copy-start(s32[16]{0:T(128)} %param.5) | copy-start | bytes 196
  36.2 15.3 %all-to-all-start = ((bf16[16,2,2048]{2,1,0:T(2,128)(2,1)}), bf16[16,2,2048]{2,1,0:T(2,128)(2,1)S(1)}, u32[]{:S(2)}, u32[]{:S(2)}) async-start(bf16[16,2,2048]{2,1,0:T(2,128)(2,1)} %reshape.8), calls=%async_computation | async-start | bytes 262144 | tf_op jit(solution)/shard_map/all_to_all | solution.py:21
  43.6 85.8 %all-gather.2.cloned.1.call-start = ((), (), s32[]{:S(2)}) async-start(), calls=%async_computation.1 | async-start | bytes 2228224 | tf_op jit(solution)/shard_map/all_gather | solution.py:36
  53.3 36.7 %copy-start = (f32[16,16,256]{2,1,0:T(8,128)S(1)}, f32[16,16,256]{2,1,0:T(8,128)}, u32[]{:S(2)}) copy-start(f32[16,16,256]{2,1,0:T(8,128)} %param.4) | copy-start | bytes 786436
Sparse Core Ops, SparseCore 0:
  91.0 38.3 all-gather.1
